TPU v7x, 32 devices: a whole 2x2x4 slice. The times are simulated.
32 devices in a mesh: fsdp: 8 (over z, y), tp: 4 (over x, core).
Axes of the slice: x: 2, y: 2, z: 4, core: 2. Of those that a mesh axis runs over, the one named last changes fastest.
Arguments:
- hidden_in: bfloat16 [1024, 8192], P('fsdp'), may hold values from -6 to 6
- key_grad: bfloat16 [1024, 1024], P('fsdp', 'tp'), may hold values from -2.5 to 2.5
- positions: int32 [1024], P('fsdp'), may hold values from 0 to 1023, as said below
- key_quant: bfloat16 [8704, 1024], P('fsdp', 'tp'), may hold values from -4 to 4
- key_scales: float32 [8704, 8], P('fsdp', 'tp'), may hold values from 0.01 to 0.1
- block_counts: int32 [8], replicated, may hold values from 960 to 1088, as said below
Outputs:
- weight_grad: bfloat16 [8704, 1024], P('fsdp', 'tp')
- input_grad: bfloat16 [1024, 8192], P('fsdp', 'tp')
Inputs may be any that keep to these rules, and one draw needn't show every extreme that they name: Index f of fsdp owns the consecutive projection rows from block_counts[0] + ... + block_counts[f-1] on, in its first block_counts[f] slots; the counts sum to 8192, and some index owns exactly 1088 rows. positions count the tokens from the start of their packed document; the first token's document may have begun before the first token, and a document may go on into the next index's tokens.
All inputs are finite; a program needn't handle non-finite values.
Results may differ from a plain program's by a relative error of at most 0.013.
Values may be sent and summed in bfloat16 or wider, within the bound.
A program may use at most 64 MiB of HBM per device.

v0:
```python
import math
import jax
import jax.numpy as jnp
from jax import lax
from jax.sharding import PartitionSpec as P

HD = 128
rope_base = 500000.0


def rotary_backward(key_grad, positions):
    tokens_here = key_grad.shape[0]
    half_dim = HD // 2
    cotangent = key_grad.astype(jnp.float32).reshape(tokens_here, -1, HD)
    freq_idx = jnp.arange(half_dim, dtype=jnp.float32)
    inverse = jnp.exp(-(2.0 * freq_idx / HD) * math.log(rope_base))
    angles = positions.astype(jnp.float32)[:, None] * inverse[None, :]
    cosine = jnp.cos(angles)[:, None, :]
    sine_part = jnp.sin(angles)[:, None, :]
    lower_half = cotangent[..., :half_dim]
    upper_half = cotangent[..., half_dim:]
    back_lower = lower_half * cosine + upper_half * sine_part
    back_upper = upper_half * cosine - lower_half * sine_part
    joined = jnp.concatenate([back_lower, back_upper], axis=-1)
    return joined.reshape(tokens_here, -1).astype(jnp.bfloat16)


def slot_tables(block_counts, slot_count, row_total):
    offsets = jnp.cumsum(block_counts) - block_counts
    owners_n = block_counts.shape[0]
    slot_ids = jnp.arange(owners_n * slot_count, dtype=jnp.int32)
    within = slot_ids % slot_count
    live_counts = jnp.broadcast_to(block_counts[:, None], (owners_n, slot_count)).reshape(-1)
    base_rows = jnp.broadcast_to(offsets[:, None], (owners_n, slot_count)).reshape(-1)
    is_live = within < live_counts
    row_of_slot = jnp.where(is_live, base_rows + within, 0)
    row_ids = jnp.arange(row_total, dtype=jnp.int32)
    at_or_after = row_ids[:, None] >= offsets[None, :]
    owner_of_row = jnp.sum(at_or_after.astype(jnp.int32), axis=1) - 1
    row_begin = jnp.max(jnp.where(at_or_after, offsets[None, :], 0), axis=1)
    slot_of_row = owner_of_row * slot_count + row_ids - row_begin
    return (row_of_slot, is_live, slot_of_row)


def per_device(hidden_in, key_grad, positions, key_quant, key_scales, block_counts):
    slot_count = key_quant.shape[0]
    local_heads = key_scales.shape[1]
    row_total = hidden_in.shape[1]
    row_of_slot, is_live, slot_of_row = slot_tables(block_counts, slot_count, row_total)
    scaled = (
        key_quant.astype(jnp.float32).reshape(slot_count, local_heads, HD) * key_scales[:, :, None]
    )
    local_weights = scaled.astype(jnp.bfloat16).reshape(slot_count, local_heads * HD)
    rotated = rotary_backward(key_grad, positions)
    picked = jnp.where(
        is_live[None, :], jnp.take(hidden_in, row_of_slot, axis=1), jnp.zeros((), jnp.bfloat16)
    )
    weight_grad = lax.psum_scatter(
        lax.dot_general(
            picked, rotated, (((0,), (0,)), ((), ())), preferred_element_type=jnp.float32
        ),
        "fsdp",
        scatter_dimension=0,
        tiled=True,
    ).astype(jnp.bfloat16)
    group_total = lax.axis_size("tp")
    whole_slots = lax.all_gather(local_weights, "fsdp", axis=0, tiled=True)
    ordered = jnp.take(whole_slots, slot_of_row, axis=0)
    own_rows = lax.all_to_all(ordered, "tp", split_axis=0, concat_axis=1, tiled=True)
    all_heads = lax.all_gather(rotated, "tp", axis=1, tiled=True)
    tokens_here = all_heads.shape[0]
    feature_here = own_rows.shape[0]
    heads_grouped = all_heads.reshape(tokens_here, group_total, -1)
    rows_grouped = own_rows.reshape(feature_here, group_total, -1)
    group_part = jnp.einsum(
        "tgk,dgk->gtd", heads_grouped, rows_grouped, preferred_element_type=jnp.float32
    ).astype(jnp.bfloat16)
    input_grad = jnp.sum(group_part.astype(jnp.float32), axis=0).astype(jnp.bfloat16)
    return (weight_grad, input_grad)


def solution(mesh):
    in_specs = (P("fsdp", None), P("fsdp", "tp"), P("fsdp"), P("fsdp", "tp"), P("fsdp", "tp"), P())
    out_specs = (P("fsdp", "tp"), P("fsdp", "tp"))
    return jax.shard_map(
        per_device, mesh=mesh, in_specs=in_specs, out_specs=out_specs, check_vma=False
    )
```

profile of v0, /device:TPU:0, one launch (start us, length us, event | category | flops | bytes accessed | tf_op | source)
XLA Modules:
  0.0 256.9 jit_solution(10514191697717490936)
XLA Ops:
  7.2 0.0 copy-start
  7.2 0.0 all-gather.2.cloned.1.call-start
  7.2 1.0 copy.18
  8.2 0.0 copy-start.2
  8.2 0.0 copy-start.1
  8.2 0.0 copy-start.3
  8.2 2.5 mul.108
  10.8 0.0 copy-done
  10.8 0.9 fusion.13
  11.7 0.0 all-gather.2.cloned.1.call-update
  11.7 0.0 reduce-scatter.2.cloned.1.call-start
  11.8 0.0 copy-done.2
  11.8 0.2 reduce-window.9
  12.0 0.1 broadcast_in_dim.67
  12.1 0.1 reshape.253
  12.2 0.1 reshape.251
  12.2 0.1 broadcast_in_dim.65
  12.3 0.1 reshape.252
  12.4 0.1 reshape.248
  12.5 0.0 copy-done.1
  12.5 0.1 copy.21
  12.6 0.0 copy-done.3
  12.6 3.2 %copy.15 = bf16[128,8192]{0,1:T(8,128)(2,1)S(1)} copy(bf16[128,8192]{1,0:T(8,128)(2,1)} %param.6) | data formatting | bytes 4194304 | tf_op args[0]
  15.9 0.2 fusion.20
  16.1 18.3 %gather_fusion = bf16[8704,128]{1,0:T(8,128)(2,1)} fusion(bf16[128,8192]{0,1:T(8,128)(2,1)S(1)} %copy.15, s32[9216]{0:T(1024)S(1)} %pad_clamp_fusion), kind=kCustom, calls=%fused_computation | custom fusion | bytes 4491264 | tf_op jit(solution)/shard_map/jit(_take)/gather | solution.py:56
  34.4 0.2 multiply_cosine_fusion
  34.7 8.8 %fusion.5 = f32[8704,256]{1,0:T(8,128)} fusion(bf16[128,256]{0,1:T(8,128)(2,1)S(1)} %bitcast.27, bf16[8704,128]{1,0:T(8,128)(2,1)} %gather_fusion, pred[8704]{0:T(1024)(128)(4,1)S(1)} %get-tuple-element.5, pred[8704]{0:T(1024)(128)(4,1)S(1)} %get-tuple-element.4), kind=kOutput, calls=%fused_computation.6 | convolution fusion | flops 572653568 | bytes 11224064 | tf_op jit(solution)/shard_map/dot_general | solution.py:59
  43.5 0.0 reduce-scatter.2.cloned.1.call-update
  43.5 0.3 convert_reduce_fusion
  43.9 0.1 compare_select_fusion.1
  44.0 46.7 %all-gather.2.cloned.1.call-done = bf16[8704,256]{1,0:T(8,128)(2,1)} async-done(((bf16[1088,256]{1,0:T(8,128)(2,1)}), bf16[8704,256]{1,0:T(8,128)(2,1)}) %all-gather.2.cloned.1.call-update) | async-done | bytes 4456464 | tf_op jit(solution)/shard_map/all_gather | solution.py:67
  90.7 33.7 %gather_fusion.1 = bf16[8192,256]{1,0:T(8,128)(2,1)} fusion(bf16[8704,256]{1,0:T(8,128)(2,1)} %all-gather.2.cloned.1.call-done, s32[8192]{0:T(1024)S(1)} %broadcast_clamp_fusion), kind=kCustom, calls=%fused_computation.1 | custom fusion | bytes 8421376 | tf_op jit(solution)/shard_map/jit(_take)/gather | solution.py:68
  124.4 5.3 %broadcast_select_fusion = bf16[4,2048,256]{2,1,0:T(8,128)(2,1)} fusion(bf16[4,2048,256]{2,1,0:T(8,128)(2,1)} %bitcast.24, pred[4,2048]{1,0:T(4,128)(4,1)S(1)} %compare_and_fusion.1), kind=kLoop, calls=%fused_computation.4 | loop fusion | flops 2097152 | bytes 8396800 | tf_op jit(solution)/shard_map/jit(_take)/select_n | solution.py:68
  129.7 4.9 %all-to-all-start = ((bf16[4,2048,256]{2,1,0:T(8,128)(2,1)}), bf16[4,2048,256]{2,1,0:T(8,128)(2,1)}, u32[]{:S(2)}, u32[]{:S(2)}) async-start(bf16[4,2048,256]{2,1,0:T(8,128)(2,1)} %broadcast_select_fusion), calls=%async_computation.1 | async-start | bytes 8388608 | tf_op jit(solution)/shard_map/all_to_all | solution.py:69
  134.6 50.3 %all_gather.6 = bf16[128,1024]{0,1:T(8,128)(2,1)S(1)} all-gather(bf16[128,256]{0,1:T(8,128)(2,1)S(1)} %bitcast.28), channel_id=1, replica_groups=mesh['fsdp'=8,'tp'=4] {'tp'}, dimensions={1}, use_global_device_ids=true | all-gather | bytes 327680 | tf_op jit(solution)/shard_map/all_gather | solution.py:70
  184.9 0.0 all-to-all-done
  184.9 4.8 %fusion.10 = bf16[128,2048]{1,0:T(8,128)(2,1)} fusion(bf16[128,4,256]{0,2,1:T(8,128)(2,1)S(1)} %bitcast.26, bf16[4,2048,256]{2,1,0:T(8,128)(2,1)} %all-to-all-done), kind=kOutput, calls=%fused_computation.11 | convolution fusion | flops 538705920 | bytes 4980736 | tf_op jit(solution)/shard_map/tgk,dgk->gtd/dot_general | solution.py:75
  189.7 58.2 %reduce-scatter.2.cloned.1.call-done = f32[1088,256]{1,0:T(8,128)} async-done(((f32[8704,256]{1,0:T(8,128)}), f32[1088,256]{1,0:T(8,128)}) %reduce-scatter.2.cloned.1.call-update) | async-done | bytes 1114128 | tf_op jit(solution)/shard_map/reduce_scatter | solution.py:58
  248.0 2.1 convert_element_type.28
  (12 shorter events, 0.2 us)
Async XLA Ops:
  7.2 3.6 %copy-start = (bf16[1088,256]{1,0:T(8,128)(2,1)S(1)}, bf16[1088,256]{1,0:T(8,128)(2,1)}, u32[]{:S(2)}) copy-start(bf16[1088,256]{1,0:T(8,128)(2,1)} %param.9) | copy-start | bytes 1671172
  7.2 83.5 %all-gather.2.cloned.1.call-start = ((), (), s32[]{:S(2)}) async-start(), calls=%async_computation.3 | async-start | bytes 5013504 | tf_op jit(solution)/shard_map/all_gather | solution.py:67
  8.2 3.6 %copy-start.2 = (s32[8]{0:T(128)S(1)}, s32[8]{0:T(128)}, u32[]{:S(2)}) copy-start(s32[8]{0:T(128)} %param.11) | copy-start | bytes 100
  8.2 4.3 %copy-start.1 = (bf16[128,256]{1,0:T(8,128)(2,1)S(1)}, bf16[128,256]{1,0:T(8,128)(2,1)}, u32[]{:S(2)}) copy-start(bf16[128,256]{1,0:T(8,128)(2,1)} %param.7) | copy-start | bytes 196612
  8.2 4.4 %copy-start.3 = (s32[128]{0:T(128)S(1)}, s32[128]{0:T(128)}, u32[]{:S(2)}) copy-start(s32[128]{0:T(128)} %param.8) | copy-start | bytes 1540
  11.7 236.3 %reduce-scatter.2.cloned.1.call-start = ((), (), s32[]{:S(2)}) async-start(), calls=%async_computation.2 | async-start | bytes 10027008 | tf_op jit(solution)/shard_map/reduce_scatter | solution.py:58
  129.7 55.2 %all-to-all-start = ((bf16[4,2048,256]{2,1,0:T(8,128)(2,1)}), bf16[4,2048,256]{2,1,0:T(8,128)(2,1)}, u32[]{:S(2)}, u32[]{:S(2)}) async-start(bf16[4,2048,256]{2,1,0:T(8,128)(2,1)} %broadcast_select_fusion), calls=%async_computation.1 | async-start | bytes 8388608 | tf_op jit(solution)/shard_map/all_to_all | solution.py:69
Sparse Core Ops, SparseCore 0:
  11.9 78.7 all-gather.1
  94.3 153.6 reduce-scatter.1
where the time goes:
time: 258 us; the launch traced here: 257 us
  waiting for transfers between devices  105 us (41%)
  local copies, waits for them, and re-layouts  59.4 us (23%)
  blocking collectives  50.3 us (19%)
  between operations  14.2 us (6%)
  matrix products  13.6 us (5%)
  other arithmetic  9.44 us (4%)
  starting transfers between devices  4.98 us (2%)
    reduce_scatter x1, waiting for transfers between devices, per_device(): lax.psum_scatter(lax.dot_general(picked, rotated, (((0,), (0,)), ((), ())...  58.2 us
    all_gather x1, blocking collectives, per_device(): all_heads = lax.all_gather(rotated, 'tp', axis=1, tiled=True)  50.3 us
    all_gather x1, waiting for transfers between devices, per_device(): whole_slots = lax.all_gather(local_weights, 'fsdp', axis=0, tiled=True)  46.7 us
    gather x1, local copies, waits for them, and re-layouts, per_device(): ordered = jnp.take(whole_slots, slot_of_row, axis=0)  33.7 us
    gather x1, local copies, waits for them, and re-layouts, per_device(): jnp.take(hidden_in, row_of_slot, axis=1)  18.3 us
    dot_general x1, matrix products, per_device(): lax.dot_general(picked, rotated, (((0,), (0,)), ((), ())), preferred_elem...  8.82 us
    select_n x2, other arithmetic, per_device(): ordered = jnp.take(whole_slots, slot_of_row, axis=0)  5.34 us
  transfers between devices with their start and end apart: 3, of which 2 were waited for; matrix products, arithmetic and copies ran while one was open for 30% of the time, Pallas kernels for 0%

commit v1 on v0

--- a/solution.py
+++ b/solution.py
@@ -6,6 +6,27 @@
 
 HD = 128
 rope_base = 500000.0
+
+
+def gather_around(array, axis, dim):
+    count, index, rows = (lax.axis_size(axis), lax.axis_index(axis), array.shape[dim])
+    right = [(i, (i + 1) % count) for i in range(count)]
+    behind = [(i, (i - 1) % count) for i in range(count)]
+    out = jnp.zeros((*array.shape[:dim], count * rows, *array.shape[dim + 1 :]), array.dtype)
+    out = lax.dynamic_update_slice_in_dim(out, array, index * rows, axis=dim)
+    from_left = from_right = array
+    half = count // 2
+    for step in range(1, half + 1):
+        from_left = lax.ppermute(from_left, axis, right)
+        out = lax.dynamic_update_slice_in_dim(
+            out, from_left, (index - step) % count * rows, axis=dim
+        )
+        if step < count - half:
+            from_right = lax.ppermute(from_right, axis, behind)
+            out = lax.dynamic_update_slice_in_dim(
+                out, from_right, (index + step) % count * rows, axis=dim
+            )
+    return out
 
 
 def rotary_backward(key_grad, positions):
@@ -64,7 +85,7 @@
         tiled=True,
     ).astype(jnp.bfloat16)
     group_total = lax.axis_size("tp")
-    whole_slots = lax.all_gather(local_weights, "fsdp", axis=0, tiled=True)
+    whole_slots = gather_around(local_weights, "fsdp", 0)
     ordered = jnp.take(whole_slots, slot_of_row, axis=0)
     own_rows = lax.all_to_all(ordered, "tp", split_axis=0, concat_axis=1, tiled=True)
     all_heads = lax.all_gather(rotated, "tp", axis=1, tiled=True)

time: 258 us -> 293 us (1.14); the launches traced: 257 us -> 289 us
  starting transfers between devices: 4.98 us -> 22 us
  local copies, waits for them, and re-layouts: 59.4 us -> 69 us
  waiting for transfers between devices: 105 us -> 108 us
    ppermute x0 -> x7, waiting for transfers between devices: none -> 108 us  [the longest x4 105 us: gather_around(): from_left = lax.ppermute(from_left, axis, right)]
    reduce_scatter x1, waiting for transfers between devices: 58.2 us -> 0.01 us  [per_device(): lax.psum_scatter(lax.dot_general(picked, rotated, (((0,), (0,)), ((), ())...]
    all_gather x1 -> x0, waiting for transfers between devices: 46.7 us -> none  [per_device(): whole_slots = lax.all_gather(local_weights, 'fsdp', axis=0, tiled=True)]
    ppermute x0 -> x7, starting transfers between devices: none -> 17.1 us  [the longest x3 11.7 us: gather_around(): from_right = lax.ppermute(from_right, axis, behind)]
    dynamic_update_slice x0 -> x7, local copies, waits for them, and re-layouts: none -> 5.93 us  [the longest x4 3.42 us: gather_around(): lax.dynamic_update_slice_in_dim(out, from_left, (index - step) % count *...]
  transfers between devices with their start and end apart: 3 -> 9, of which waited for: 2 -> 6; matrix products, arithmetic and copies ran while one was open for 30% -> 19% of each run, Pallas kernels for 0% -> 0%
where the time goes in v1:
time: 293 us; the launch traced here: 289 us
  waiting for transfers between devices  108 us (37%)
  local copies, waits for them, and re-layouts  69 us (24%)
  blocking collectives  50.3 us (17%)
  starting transfers between devices  22 us (8%)
  between operations  14.2 us (5%)
  matrix products  13.4 us (5%)
  other arithmetic  11.7 us (4%)
    ppermute x4, waiting for transfers between devices, gather_around(): from_left = lax.ppermute(from_left, axis, right)  105 us
    all_gather x1, blocking collectives, per_device(): all_heads = lax.all_gather(rotated, 'tp', axis=1, tiled=True)  50.3 us
    gather x1, local copies, waits for them, and re-layouts, per_device(): ordered = jnp.take(whole_slots, slot_of_row, axis=0)  33.7 us
    gather x1, local copies, waits for them, and re-layouts, per_device(): jnp.take(hidden_in, row_of_slot, axis=1)  18.3 us
    ppermute x3, starting transfers between devices, gather_around(): from_right = lax.ppermute(from_right, axis, behind)  11.7 us
    dot_general x1, matrix products, per_device(): lax.dot_general(picked, rotated, (((0,), (0,)), ((), ())), preferred_elem...  8.8 us
  transfers between devices with their start and end apart: 9, of which 6 were waited for; matrix products, arithmetic and copies ran while one was open for 19% of the time, Pallas kernels for 0%

profile of v1, /device:TPU:0, one launch (start us, length us, event | category | flops | bytes accessed | tf_op | source)
XLA Modules:
  0.0 288.7 jit_solution(4815059940981942307)
XLA Ops:
  7.2 0.0 reduce-scatter.2.cloned.1.call-start
  7.2 0.8 reduce-window.9
  8.1 0.7 bitcast_subtract_fusion
  8.7 0.1 broadcast_in_dim.70
  8.8 0.1 reshape.253
  8.9 0.1 reshape.251
  9.0 0.7 broadcast_in_dim.68
  9.7 0.1 reshape.252
  9.8 0.1 reshape.248
  9.9 0.9 copy.21
  10.8 0.7 convert_element_type.26
  11.5 3.2 %copy.15 = bf16[128,8192]{0,1:T(8,128)(2,1)S(1)} copy(bf16[128,8192]{1,0:T(8,128)(2,1)} %param.6) | data formatting | bytes 4194304 | tf_op args[0]
  14.7 0.2 fusion.20
  15.0 0.2 multiply_cosine_fusion
  15.2 18.3 %gather_fusion = bf16[8704,128]{1,0:T(8,128)(2,1)} fusion(bf16[128,8192]{0,1:T(8,128)(2,1)S(1)} %copy.15, s32[9216]{0:T(1024)S(1)} %pad_clamp_fusion), kind=kCustom, calls=%fused_computation | custom fusion | bytes 4491264 | tf_op jit(solution)/shard_map/jit(_take)/gather | solution.py:77
  33.5 8.8 %fusion.5 = f32[8704,256]{1,0:T(8,128)} fusion(bf16[128,256]{0,1:T(8,128)(2,1)S(1)} %bitcast.28, bf16[8704,128]{1,0:T(8,128)(2,1)} %gather_fusion, pred[8704]{0:T(1024)(128)(4,1)S(1)} %get-tuple-element.7, pred[8704]{0:T(1024)(128)(4,1)S(1)} %get-tuple-element.6), kind=kOutput, calls=%fused_computation.6 | convolution fusion | flops 572653568 | bytes 11224064 | tf_op jit(solution)/shard_map/dot_general | solution.py:80
  42.4 0.0 reduce-scatter.2.cloned.1.call-update
  42.4 0.7 copy-done.1
  43.0 0.2 copy.18
  43.3 2.5 mul.132
  45.8 2.3 broadcast_in_dim.76
  48.1 1.1 constant_dynamic-update-slice_fusion.7
  49.2 2.9 %collective-permute-start = (bf16[1088,256]{1,0:T(8,128)(2,1)S(1)}, bf16[1088,256]{1,0:T(8,128)(2,1)S(1)}, u32[]{:S(2)}, u32[]{:S(2)}) collective-permute-start(bf16[1088,256]{1,0:T(8,128)(2,1)S(1)} %get-tuple-element.5), channel_id=1, source_target_pairs={{0,4},{4,8},{8,12},{12,16},{16,20},{20,24},{24,28},{28,0},{1,5},{5... | collective-permute-start | bytes 1671176 | tf_op jit(solution)/shard_map/ppermute | solution.py:20
  52.1 3.1 %collective-permute-start.1 = (bf16[1088,256]{1,0:T(8,128)(2,1)S(1)}, bf16[1088,256]{1,0:T(8,128)(2,1)S(1)}, u32[]{:S(2)}, u32[]{:S(2)}) collective-permute-start(bf16[1088,256]{1,0:T(8,128)(2,1)S(1)} %get-tuple-element.5), channel_id=1, source_target_pairs={{0,28},{4,0},{8,4},{12,8},{16,12},{20,16},{24,20},{28,24},{1,29},{... | collective-permute-start | bytes 1671176 | tf_op jit(solution)/shard_map/ppermute | solution.py:25
  55.2 0.3 convert_reduce_fusion
  55.5 0.1 compare_select_fusion.1
  55.6 32.3 %collective-permute-done = bf16[1088,256]{1,0:T(8,128)(2,1)S(1)} collective-permute-done((bf16[1088,256]{1,0:T(8,128)(2,1)S(1)}, bf16[1088,256]{1,0:T(8,128)(2,1)S(1)}, u32[]{:S(2)}, u32[]{:S(2)}) %collective-permute-start) | collective-permute-done | bytes 557088 | tf_op jit(solution)/shard_map/ppermute | solution.py:20
  87.8 2.5 collective-permute-start.2
  90.4 3.1 %collective-permute-start.3 = (bf16[1088,256]{1,0:T(8,128)(2,1)S(1)}, bf16[1088,256]{1,0:T(8,128)(2,1)S(1)}, u32[]{:S(2)}, u32[]{:S(2)}) collective-permute-start(bf16[1088,256]{1,0:T(8,128)(2,1)S(1)} %collective-permute-done.1), channel_id=1, source_target_pairs={{0,28},{4,0},{8,4},{12,8},{16,12},{20,16},{24,20},{28,24},{1,29},{... | collective-permute-start | bytes 1671176 | tf_op jit(solution)/shard_map/ppermute | solution.py:25
  93.5 24.1 %collective-permute-done.2 = bf16[1088,256]{1,0:T(8,128)(2,1)S(1)} collective-permute-done((bf16[1088,256]{1,0:T(8,128)(2,1)S(1)}, bf16[1088,256]{1,0:T(8,128)(2,1)S(1)}, u32[]{:S(2)}, u32[]{:S(2)}) %collective-permute-start.2) | collective-permute-done | bytes 557088 | tf_op jit(solution)/shard_map/ppermute | solution.py:20
  117.6 0.9 constant_dynamic-update-slice_fusion.6
  118.5 0.8 constant_dynamic-update-slice_fusion.5
  119.3 1.3 collective-permute-done.3
  120.6 5.4 %collective-permute-start.5 = (bf16[1088,256]{1,0:T(8,128)(2,1)S(1)}, bf16[1088,256]{1,0:T(8,128)(2,1)S(1)}, u32[]{:S(2)}, u32[]{:S(2)}) collective-permute-start(bf16[1088,256]{1,0:T(8,128)(2,1)S(1)} %collective-permute-done.3), channel_id=1, source_target_pairs={{0,28},{4,0},{8,4},{12,8},{16,12},{20,16},{24,20},{28,24},{1,29},{... | collective-permute-start | bytes 1671176 | tf_op jit(solution)/shard_map/ppermute | solution.py:25
  126.1 0.8 constant_dynamic-update-slice_fusion.4
  126.9 21.0 %collective-permute-done.4 = bf16[1088,256]{1,0:T(8,128)(2,1)S(1)} collective-permute-done((bf16[1088,256]{1,0:T(8,128)(2,1)S(1)}, bf16[1088,256]{1,0:T(8,128)(2,1)S(1)}, u32[]{:S(2)}, u32[]{:S(2)}) %collective-permute-start.4) | collective-permute-done | bytes 557088 | tf_op jit(solution)/shard_map/ppermute | solution.py:20
  147.9 0.8 constant_dynamic-update-slice_fusion.3
  148.8 0.9 constant_dynamic-update-slice_fusion.2
  149.6 2.1 collective-permute-done.5
  151.7 0.9 constant_dynamic-update-slice_fusion.1
  152.6 27.3 %collective-permute-done.6 = bf16[1088,256]{1,0:T(8,128)(2,1)S(1)} collective-permute-done((bf16[1088,256]{1,0:T(8,128)(2,1)S(1)}, bf16[1088,256]{1,0:T(8,128)(2,1)S(1)}, u32[]{:S(2)}, u32[]{:S(2)}) %collective-permute-start.6) | collective-permute-done | bytes 557088 | tf_op jit(solution)/shard_map/ppermute | solution.py:20
  179.9 0.8 constant_dynamic-update-slice_fusion
  180.7 33.7 %gather_fusion.1 = bf16[8192,256]{1,0:T(8,128)(2,1)} fusion(bf16[8704,256]{1,0:T(8,128)(2,1)} %constant_dynamic-update-slice_fusion, s32[8192]{0:T(1024)S(1)} %broadcast_clamp_fusion), kind=kCustom, calls=%fused_computation.1 | custom fusion | bytes 8421376 | tf_op jit(solution)/shard_map/jit(_take)/gather | solution.py:89
  214.4 5.5 %broadcast_select_fusion = bf16[4,2048,256]{2,1,0:T(8,128)(2,1)} fusion(bf16[4,2048,256]{2,1,0:T(8,128)(2,1)} %bitcast.25, pred[4,2048]{1,0:T(4,128)(4,1)S(1)} %compare_and_fusion.1), kind=kLoop, calls=%fused_computation.4 | loop fusion | flops 2097152 | bytes 8396800 | tf_op jit(solution)/shard_map/jit(_take)/select_n | solution.py:89
  219.9 4.9 %all-to-all-start = ((bf16[4,2048,256]{2,1,0:T(8,128)(2,1)}), bf16[4,2048,256]{2,1,0:T(8,128)(2,1)}, u32[]{:S(2)}, u32[]{:S(2)}) async-start(bf16[4,2048,256]{2,1,0:T(8,128)(2,1)} %broadcast_select_fusion), calls=%async_computation.1 | async-start | bytes 8388608 | tf_op jit(solution)/shard_map/all_to_all | solution.py:90
  224.8 50.3 %all_gather.3 = bf16[128,1024]{0,1:T(8,128)(2,1)S(1)} all-gather(bf16[128,256]{0,1:T(8,128)(2,1)S(1)} %bitcast.29), channel_id=1, replica_groups=mesh['fsdp'=8,'tp'=4] {'tp'}, dimensions={1}, use_global_device_ids=true | all-gather | bytes 327680 | tf_op jit(solution)/shard_map/all_gather | solution.py:91
  275.2 4.6 %fusion.10 = bf16[128,2048]{1,0:T(8,128)(2,1)} fusion(bf16[128,4,256]{0,2,1:T(8,128)(2,1)S(1)} %bitcast.27, bf16[4,2048,256]{2,1,0:T(8,128)(2,1)} %all-to-all-done), kind=kOutput, calls=%fused_computation.11 | convolution fusion | flops 538705920 | bytes 4980736 | tf_op jit(solution)/shard_map/tgk,dgk->gtd/dot_general | solution.py:96
  279.8 2.1 convert_element_type.28
  (18 shorter events, 0.2 us)
Async XLA Ops:
  7.2 272.6 %reduce-scatter.2.cloned.1.call-start = ((), (), s32[]{:S(2)}) async-start(), calls=%async_computation.2 | async-start | bytes 10027008 | tf_op jit(solution)/shard_map/reduce_scatter | solution.py:79
  42.3 0.7 copy-start.1
  42.4 5.7 %copy-start = (bf16[1088,256]{1,0:T(8,128)(2,1)S(1)}, bf16[1088,256]{1,0:T(8,128)(2,1)}, u32[]{:S(2)}) copy-start(bf16[1088,256]{1,0:T(8,128)(2,1)} %param.9) | copy-start | bytes 1671172
  49.2 38.7 %collective-permute-start = (bf16[1088,256]{1,0:T(8,128)(2,1)S(1)}, bf16[1088,256]{1,0:T(8,128)(2,1)S(1)}, u32[]{:S(2)}, u32[]{:S(2)}) collective-permute-start(bf16[1088,256]{1,0:T(8,128)(2,1)S(1)} %get-tuple-element.5), channel_id=1, source_target_pairs={{0,4},{4,8},{8,12},{12,16},{16,20},{20,24},{24,28},{28,0},{1,5},{5... | collective-permute-start | bytes 1671176 | tf_op jit(solution)/shard_map/ppermute | solution.py:20
  52.1 38.3 %collective-permute-start.1 = (bf16[1088,256]{1,0:T(8,128)(2,1)S(1)}, bf16[1088,256]{1,0:T(8,128)(2,1)S(1)}, u32[]{:S(2)}, u32[]{:S(2)}) collective-permute-start(bf16[1088,256]{1,0:T(8,128)(2,1)S(1)} %get-tuple-element.5), channel_id=1, source_target_pairs={{0,28},{4,0},{8,4},{12,8},{16,12},{20,16},{24,20},{28,24},{1,29},{... | collective-permute-start | bytes 1671176 | tf_op jit(solution)/shard_map/ppermute | solution.py:25
  87.8 29.8 %collective-permute-start.2 = (bf16[1088,256]{1,0:T(8,128)(2,1)S(1)}, bf16[1088,256]{1,0:T(8,128)(2,1)S(1)}, u32[]{:S(2)}, u32[]{:S(2)}) collective-permute-start(bf16[1088,256]{1,0:T(8,128)(2,1)S(1)} %collective-permute-done), channel_id=1, source_target_pairs={{0,4},{4,8},{8,12},{12,16},{16,20},{20,24},{24,28},{28,0},{1,5},{5... | collective-permute-start | bytes 1671176 | tf_op jit(solution)/shard_map/ppermute | solution.py:20
  90.4 30.3 %collective-permute-start.3 = (bf16[1088,256]{1,0:T(8,128)(2,1)S(1)}, bf16[1088,256]{1,0:T(8,128)(2,1)S(1)}, u32[]{:S(2)}, u32[]{:S(2)}) collective-permute-start(bf16[1088,256]{1,0:T(8,128)(2,1)S(1)} %collective-permute-done.1), channel_id=1, source_target_pairs={{0,28},{4,0},{8,4},{12,8},{16,12},{20,16},{24,20},{28,24},{1,29},{... | collective-permute-start | bytes 1671176 | tf_op jit(solution)/shard_map/ppermute | solution.py:25
  117.6 30.3 %collective-permute-start.4 = (bf16[1088,256]{1,0:T(8,128)(2,1)S(1)}, bf16[1088,256]{1,0:T(8,128)(2,1)S(1)}, u32[]{:S(2)}, u32[]{:S(2)}) collective-permute-start(bf16[1088,256]{1,0:T(8,128)(2,1)S(1)} %collective-permute-done.2), channel_id=1, source_target_pairs={{0,4},{4,8},{8,12},{12,16},{16,20},{20,24},{24,28},{28,0},{1,5},{5... | collective-permute-start | bytes 1671176 | tf_op jit(solution)/shard_map/ppermute | solution.py:20
  120.6 31.1 %collective-permute-start.5 = (bf16[1088,256]{1,0:T(8,128)(2,1)S(1)}, bf16[1088,256]{1,0:T(8,128)(2,1)S(1)}, u32[]{:S(2)}, u32[]{:S(2)}) collective-permute-start(bf16[1088,256]{1,0:T(8,128)(2,1)S(1)} %collective-permute-done.3), channel_id=1, source_target_pairs={{0,28},{4,0},{8,4},{12,8},{16,12},{20,16},{24,20},{28,24},{1,29},{... | collective-permute-start | bytes 1671176 | tf_op jit(solution)/shard_map/ppermute | solution.py:25
  147.9 31.9 %collective-permute-start.6 = (bf16[1088,256]{1,0:T(8,128)(2,1)S(1)}, bf16[1088,256]{1,0:T(8,128)(2,1)S(1)}, u32[]{:S(2)}, u32[]{:S(2)}) collective-permute-start(bf16[1088,256]{1,0:T(8,128)(2,1)S(1)} %collective-permute-done.4), channel_id=1, source_target_pairs={{0,4},{4,8},{8,12},{12,16},{16,20},{20,24},{24,28},{28,0},{1,5},{5... | collective-permute-start | bytes 1671176 | tf_op jit(solution)/shard_map/ppermute | solution.py:20
  219.9 55.2 %all-to-all-start = ((bf16[4,2048,256]{2,1,0:T(8,128)(2,1)}), bf16[4,2048,256]{2,1,0:T(8,128)(2,1)}, u32[]{:S(2)}, u32[]{:S(2)}) async-start(bf16[4,2048,256]{2,1,0:T(8,128)(2,1)} %broadcast_select_fusion), calls=%async_computation.1 | async-start | bytes 8388608 | tf_op jit(solution)/shard_map/all_to_all | solution.py:90
Sparse Core Ops, SparseCore 0:
  42.5 213.0 reduce-scatter.1
